TPU v7x, 128 devices: a whole 4x4x4 slice. The times are simulated.
128 devices in a mesh: expert: 8 (over z, core), fsdp: 16 (over y, x).
Axes of the slice: x: 4, y: 4, z: 4, core: 2. Of those that a mesh axis runs over, the one named last changes fastest.
Arguments:
- hidden: bfloat16 [8, 768, 8192], P('expert', None, 'fsdp'), may hold values from -0.198873782 to 0.198873782
- expert_ids: int32 [2048, 2], P(('expert', 'fsdp')), may hold values from 0 to 7, all different within a row; in each aligned block of 16 rows (0 to 15, 16 to 31, ...) at most 6 rows name the same one
- gate_weights: float32 [2048, 2], P(('expert', 'fsdp')), may hold values from 0.2 to 1
- loss_weight: float32 [2048], P(('expert', 'fsdp')), may hold values from 0.3 to 3
- decay: float32 [1], replicated, may hold values from 0.2 to 0.6
- val_grad: bfloat16 [8, 8192, 4096], P('expert', 'fsdp'), may hold values from -8 to 8
- down_weight: bfloat16 [8, 8192, 4096], P('expert', 'fsdp'), may hold values from -0.0625 to 0.0625
Outputs:
- solution: float32 [8, 8192, 4096], P('expert', 'fsdp')
- hyper: float32 [1], replicated
Inputs may be any that keep to these rules, and one draw needn't show every extreme that they name: `expert_ids`: each token names 2 different experts; among the 16 tokens of one device no expert is named more than 6 times, a bound that some block reaches.
All inputs are finite; a program needn't handle non-finite values.
Results may differ from a plain program's by a relative error of at most 0.00067.
Values may be sent and summed in bfloat16 or wider, within the bound.
No kernel may reach another device: no remote copies, remote signals or barrier semaphores. Data moves between devices by JAX's collectives and lax.ppermute only.
A program may use at most 128 MiB of HBM per device.

v0:
```python
import math
import jax
import jax.numpy as jnp
from jax import lax
from jax.sharding import Mesh
from jax.sharding import PartitionSpec as P

D = 4096
ITERS = 2
EXPERT_FSDP = ("expert_0", "expert_1", "fsdp_0", "fsdp_1")
EXPERT = ("expert_0", "expert_1")
FSDP = ("fsdp_0", "fsdp_1")


def by_axis(array, axes):
    for axis in axes:
        array = lax.psum(array, axis)
    return array


def gate_table(expert_ids, gate_weights, experts, capacity):
    flat_ids = expert_ids.reshape(-1)
    labels = jnp.arange(experts, dtype=jnp.int32)
    onehot = (flat_ids[:, None] == labels[None, :]).astype(jnp.int32)
    earlier = jnp.cumsum(onehot, axis=0) - onehot
    slots = jnp.sum(earlier * onehot, axis=1)
    targets = flat_ids * capacity + slots
    columns = jnp.arange(experts * capacity, dtype=jnp.int32)
    hits = (targets[:, None] == columns[None, :]).astype(jnp.float32)
    weighted = hits * gate_weights.reshape(-1)[:, None]
    return jnp.sum(weighted.reshape(-1, expert_ids.shape[1], experts * capacity), axis=1)


def combine(table, weights, outputs):
    mixed = jnp.dot(
        table, outputs, precision=lax.Precision.HIGHEST, preferred_element_type=jnp.float32
    )
    scaled = weights[:, None] * mixed
    back = jnp.dot(
        table.T, scaled, precision=lax.Precision.HIGHEST, preferred_element_type=jnp.float32
    )
    return back.astype(jnp.bfloat16)


def joined_sums(residual, direction, image, target):
    return (
        by_axis(jnp.sum(residual * residual), EXPERT_FSDP),
        by_axis(jnp.sum(direction * image), EXPERT_FSDP),
        by_axis(jnp.sum(residual * image), EXPERT_FSDP),
        by_axis(jnp.sum(image * image), EXPERT_FSDP),
        by_axis(jnp.sum(target.astype(jnp.float32) * direction), EXPERT_FSDP),
    )


def local(hidden, expert_ids, gate_weights, loss_weight, decay, val_grad, down_weight):
    n_expert = lax.axis_size(EXPERT)
    n_fsdp = lax.axis_size(FSDP)
    capacity = hidden.shape[1] // (n_expert * n_fsdp)
    decay_rate = decay[0]
    table = gate_table(expert_ids, gate_weights, n_expert, capacity)
    local_hidden = hidden[0]
    right_side, target = (val_grad, down_weight)
    start_side = right_side.astype(jnp.float32)
    solution = jnp.zeros_like(start_side)
    residual = start_side
    direction = start_side
    along_total = jnp.float32(0.0)
    for iteration in range(ITERS):
        if iteration > 0:
            direction = residual + norm_guess / norm_prev * direction
        rounded = direction[0].astype(jnp.bfloat16)
        summed = lax.psum_scatter(
            jnp.dot(local_hidden, rounded, preferred_element_type=jnp.float32),
            FSDP,
            scatter_dimension=0,
            tiled=True,
        )
        arrived = lax.all_to_all(summed, EXPERT, split_axis=0, concat_axis=0, tiled=True)
        leaving = combine(table, loss_weight, arrived)
        returned = lax.all_to_all(leaving, EXPERT, split_axis=0, concat_axis=0, tiled=True)
        gradient = lax.dot_general(
            local_hidden,
            lax.all_gather(returned, FSDP, axis=0, tiled=True),
            (((0,), (0,)), ((), ())),
            preferred_element_type=jnp.float32,
        )
        image = gradient[None] + decay_rate * direction
        norm_now, curve, cross, square, along = joined_sums(residual, direction, image, target)
        alpha = norm_now / curve
        solution = solution + alpha * direction
        residual = residual - alpha * image
        norm_guess = norm_now - 2.0 * alpha * cross + alpha * alpha * square
        norm_prev = norm_now
        along_total = along_total + alpha * along
    hyper = -along_total / math.sqrt(n_expert * D)
    return (solution, jnp.reshape(hyper, (1,)))


def solution(mesh):
    finer = Mesh(mesh.devices.reshape(4, 2, 4, 4), ("expert_0", "expert_1", "fsdp_0", "fsdp_1"))
    placed = (
        P(EXPERT, None, FSDP),
        P(EXPERT_FSDP, None),
        P(EXPERT_FSDP, None),
        P(EXPERT_FSDP),
        P(),
        P(EXPERT, FSDP, None),
        P(EXPERT, FSDP, None),
    )
    return jax.shard_map(
        local, mesh=finer, in_specs=placed, out_specs=(P(EXPERT, FSDP, None), P()), check_vma=False
    )
```

profile of v0, /device:TPU:0, one launch (start us, length us, event | category | flops | bytes accessed | tf_op | source)
XLA Modules:
  0.0 544.2 jit_solution(16271983358100491739)
XLA Ops:
  7.2 1.1 copy-done
  8.3 8.6 %fusion.10 = f32[768,4096]{1,0:T(8,128)} fusion(bf16[1,512,4096]{2,1,0:T(8,128)(2,1)} %param.12, bf16[1,768,512]{2,1,0:T(8,128)(2,1)S(1)} %copy-done), kind=kOutput, calls=%fused_computation.26 | convolution fusion | flops 3221225472 | bytes 17563648 | tf_op jit(solution)/shard_map/dot_general | solution.py:73
  16.9 97.7 %reduce-scatter.5.cloned.1.call-done = f32[48,4096]{1,0:T(8,128)} async-done(((f32[768,4096]{1,0:T(8,128)}), f32[48,4096]{1,0:T(8,128)}) %reduce-scatter.5.cloned.1.call-update) | async-done | bytes 786448 | tf_op jit(solution)/shard_map/reduce_scatter | solution.py:72
  114.5 2.2 all_to_all.32
  116.7 4.4 all-to-all-start
  121.2 0.1 copy.41
  121.3 0.1 eq.29
  121.4 0.1 fusion.17
  121.5 0.1 reduce_window_sum.11
  121.5 0.2 select_reduce_fusion.1
  121.7 0.1 reduce_sum.89
  121.8 0.1 copy.42
  121.9 0.1 select_reduce_fusion
  122.0 15.1 %all-to-all-done = f32[8,6,4096]{2,1,0:T(8,128)S(1)} async-done(((f32[8,6,4096]{2,1,0:T(8,128)}), f32[8,6,4096]{2,1,0:T(8,128)S(1)}, u32[]{:S(2)}, u32[]{:S(2)}) %all-to-all-start) | async-done | bytes 786464 | tf_op jit(solution)/shard_map/all_to_all | solution.py:78
  137.1 0.1 all_to_all.34
  137.2 0.5 convolution_multiply_fusion.1
  137.7 0.8 convolution_convert_fusion.1
  138.6 0.1 all_to_all.35
  138.7 12.8 %all_to_all.48 = bf16[8,6,4096]{2,1,0:T(8,128)(2,1)S(1)} all-to-all(bf16[8,6,4096]{2,1,0:T(8,128)(2,1)S(1)} %all_to_all.35), channel_id=1, replica_groups=mesh['expert_0'=4,'expert_1'=2,'fsdp_0'=4,'fsdp_1'=4] {'expert_0','exper..., dimensions={0} | all-to-all | bytes 786432 | tf_op jit(solution)/shard_map/all_to_all | solution.py:80
  151.5 0.9 all_to_all.37
  152.4 6.5 %copy.40 = bf16[1,512,4096]{1,2,0:T(8,128)(2,1)} copy(bf16[1,512,4096]{2,1,0:T(8,128)(2,1)} %param.12) | data formatting | bytes 8388608 | tf_op args[5]
  159.6 51.1 %all-gather.3.cloned.1.call-done = bf16[768,4096]{1,0:T(8,128)(2,1)} async-done(((bf16[48,4096]{1,0:T(8,128)(2,1)}), bf16[768,4096]{1,0:T(8,128)(2,1)}) %all-gather.3.cloned.1.call-update) | async-done | bytes 6291472 | tf_op jit(solution)/shard_map/all_gather | solution.py:83
  210.7 12.3 %multiply_reduce_fusion = (f32[]{:T(128)}, f32[]{:T(128)}, f32[]{:T(128)}, f32[1,512,4096]{1,2,0:T(8,128)}) fusion(bf16[1,512,4096]{1,2,0:T(8,128)(2,1)} %copy.40, f32[]{:T(128)} %bitcast.44, bf16[768,4096]{1,0:T(8,128)(2,1)} %all-gather.3.cloned.1.call-done, bf16[1,768,512]{2,1,0:T(8,128)(2,1)S(1)} %copy-done), kind=kOutput, calls=%fused_computation.18 | convolution fusion | flops 3240099840 | bytes 19660816 | tf_op jit(solution)/shard_map/dot_general | solution.py:81
  222.9 11.4 %all-reduce.5 = (f32[]{:T(128)}, f32[]{:T(128)}, f32[]{:T(128)}) all-reduce(f32[]{:T(128)} %get-tuple-element.17, f32[]{:T(128)} %get-tuple-element.16, f32[]{:T(128)} %get-tuple-element.15), channel_id=1, replica_groups=mesh['expert_0'=4,'expert_1'=2,'fsdp_0'=4,'fsdp_1'=4] {'expert_0'}, use_global_device_ids=true, to_apply=%region_1.2 | all-reduce | flops 3 | bytes 24 | tf_op jit(solution)/shard_map/psum | solution.py:17
  234.3 3.1 all-reduce.7
  237.4 11.1 %all-reduce.3 = (f32[]{:T(128)}, f32[]{:T(128)}, f32[]{:T(128)}) all-reduce(f32[]{:T(128)} %get-tuple-element.43, f32[]{:T(128)} %get-tuple-element.44, f32[]{:T(128)} %get-tuple-element.45), channel_id=1, replica_groups=mesh['expert_0'=4,'expert_1'=2,'fsdp_0'=4,'fsdp_1'=4] {'fsdp_0'}, use_global_device_ids=true, to_apply=%region_3.4 | all-reduce | flops 3 | bytes 24 | tf_op jit(solution)/shard_map/psum | solution.py:17
  248.5 9.4 %all-reduce.1 = (f32[]{:T(128)}, f32[]{:T(128)}, f32[]{:T(128)}) all-reduce(f32[]{:T(128)} %get-tuple-element.29, f32[]{:T(128)} %get-tuple-element.30, f32[]{:T(128)} %get-tuple-element.31), channel_id=1, replica_groups=mesh['expert_0'=4,'expert_1'=2,'fsdp_0'=4,'fsdp_1'=4] {'fsdp_1'}, use_global_device_ids=true, to_apply=%region_4.5 | all-reduce | flops 3 | bytes 24 | tf_op jit(solution)/shard_map/psum | solution.py:17
  261.8 13.1 %convolution_bitcast_fusion = f32[768,4096]{0,1:T(8,128)} fusion(bf16[1,768,512]{2,1,0:T(8,128)(2,1)S(1)} %copy-done, bf16[1,512,4096]{1,2,0:T(8,128)(2,1)} %copy.40, f32[1,512,4096]{1,2,0:T(8,128)} %get-tuple-element.46, f32[]{:T(128)S(6)} %div.13, f32[]{:T(128)S(6)} %div.12), kind=kOutput, calls=%fused_computation.20 | convolution fusion | flops 3233808384 | bytes 25952264 | tf_op jit(solution)/shard_map/dot_general | solution.py:73
  274.9 12.6 %copy.46 = f32[768,4096]{1,0:T(8,128)} copy(f32[768,4096]{0,1:T(8,128)} %convolution_bitcast_fusion) | data formatting | bytes 25165824
  287.6 89.8 %reduce-scatter.7.cloned.1.call-done = f32[48,4096]{1,0:T(8,128)} async-done(((f32[768,4096]{1,0:T(8,128)}), f32[48,4096]{1,0:T(8,128)}) %reduce-scatter.7.cloned.1.call-update) | async-done | bytes 786448 | tf_op jit(solution)/shard_map/reduce_scatter | solution.py:72
  377.4 1.2 all_to_all.38
  378.6 20.2 %all_to_all.49 = f32[8,6,4096]{2,1,0:T(8,128)S(1)} all-to-all(f32[8,6,4096]{2,1,0:T(8,128)S(1)} %all_to_all.38), channel_id=1, replica_groups=mesh['expert_0'=4,'expert_1'=2,'fsdp_0'=4,'fsdp_1'=4] {'expert_0','exper..., dimensions={0} | all-to-all | bytes 1572864 | tf_op jit(solution)/shard_map/all_to_all | solution.py:78
  398.8 0.1 all_to_all.40
  398.9 0.5 convolution_multiply_fusion
  399.4 0.8 convolution_convert_fusion
  400.2 0.1 all_to_all.41
  400.4 12.8 %all_to_all.50 = bf16[8,6,4096]{2,1,0:T(8,128)(2,1)S(1)} all-to-all(bf16[8,6,4096]{2,1,0:T(8,128)(2,1)S(1)} %all_to_all.41), channel_id=1, replica_groups=mesh['expert_0'=4,'expert_1'=2,'fsdp_0'=4,'fsdp_1'=4] {'expert_0','exper..., dimensions={0} | all-to-all | bytes 786432 | tf_op jit(solution)/shard_map/all_to_all | solution.py:80
  413.1 0.9 all_to_all.43
  414.1 6.6 %copy.44 = bf16[1,512,4096]{1,2,0:T(8,128)(2,1)} copy(bf16[1,512,4096]{2,1,0:T(8,128)(2,1)} %param.13) | data formatting | bytes 8388608 | tf_op args[6]
  420.7 8.4 %fusion = (f32[]{:T(128)}, f32[]{:T(128)}, f32[]{:T(128)}) fusion(bf16[1,512,4096]{1,2,0:T(8,128)(2,1)} %copy.44, f32[]{:T(128)S(6)} %div.13, f32[1,512,4096]{1,2,0:T(8,128)} %get-tuple-element.46, f32[]{:T(128)S(6)} %div.12, bf16[1,512,4096]{1,2,0:T(8,128)(2,1)} %copy.40), kind=kLoop, calls=%fused_computation.8 | loop fusion | flops 25165824 | bytes 16777236 | tf_op jit(solution)/shard_map/reduce_sum | solution.py:51
  429.0 43.4 %all-gather.5.cloned.1.call-done = bf16[768,4096]{1,0:T(8,128)(2,1)} async-done(((bf16[48,4096]{1,0:T(8,128)(2,1)}), bf16[768,4096]{1,0:T(8,128)(2,1)}) %all-gather.5.cloned.1.call-update) | async-done | bytes 6291472 | tf_op jit(solution)/shard_map/all_gather | solution.py:83
  472.4 10.1 %fusion.8 = f32[]{:T(128)} fusion(bf16[768,4096]{1,0:T(8,128)(2,1)} %all-gather.5.cloned.1.call-done, f32[]{:T(128)} %bitcast.45, bf16[1,768,512]{2,1,0:T(8,128)(2,1)S(1)} %copy-done, f32[]{:T(128)S(6)} %div.13, f32[1,512,4096]{1,2,0:T(8,128)} %get-tuple-element.46, f32[]{:T(128)S(6)} %div.12, bf16[1,512,4096]{1,2,0:T(8,128)(2,1)} %copy.40), kind=kOutput, calls=%fused_computation.17 | convolution fusion | flops 3240099840 | bytes 19660816 | tf_op jit(solution)/shard_map/dot_general | solution.py:81
  482.5 11.4 %all-reduce.4 = (f32[]{:T(128)}, f32[]{:T(128)}, f32[]{:T(128)}, f32[]{:T(128)}) all-reduce(f32[]{:T(128)} %get-tuple-element.13, f32[]{:T(128)} %fusion.8, f32[]{:T(128)} %get-tuple-element.14, f32[]{:T(128)} %get-tuple-element.12), channel_id=1, replica_groups=mesh['expert_0'=4,'expert_1'=2,'fsdp_0'=4,'fsdp_1'=4] {'expert_0'}, use_global_device_ids=true, to_apply=%region_15.16 | all-reduce | flops 4 | bytes 32 | tf_op jit(solution)/shard_map/psum | solution.py:17
  493.9 3.2 all-reduce.6
  497.0 11.1 %all-reduce.2 = (f32[]{:T(128)}, f32[]{:T(128)}, f32[]{:T(128)}, f32[]{:T(128)}) all-reduce(f32[]{:T(128)} %get-tuple-element.39, f32[]{:T(128)} %get-tuple-element.40, f32[]{:T(128)} %get-tuple-element.41, f32[]{:T(128)} %get-tuple-element.42), channel_id=1, replica_groups=mesh['expert_0'=4,'expert_1'=2,'fsdp_0'=4,'fsdp_1'=4] {'fsdp_0'}, use_global_device_ids=true, to_apply=%region_17.18 | all-reduce | flops 4 | bytes 32 | tf_op jit(solution)/shard_map/psum | solution.py:17
  508.1 9.2 %all-reduce = (f32[]{:T(128)}, f32[]{:T(128)}, f32[]{:T(128)}, f32[]{:T(128)}) all-reduce(f32[]{:T(128)} %get-tuple-element.25, f32[]{:T(128)} %get-tuple-element.26, f32[]{:T(128)} %get-tuple-element.27, f32[]{:T(128)} %get-tuple-element.28), channel_id=1, replica_groups=mesh['expert_0'=4,'expert_1'=2,'fsdp_0'=4,'fsdp_1'=4] {'fsdp_1'}, use_global_device_ids=true, to_apply=%region_18.19 | all-reduce | flops 4 | bytes 32 | tf_op jit(solution)/shard_map/psum | solution.py:17
  518.7 7.7 %fusion.4 = f32[1,512,4096]{1,2,0:T(8,128)} fusion(bf16[1,512,4096]{1,2,0:T(8,128)(2,1)} %copy.40, f32[]{:T(128)S(6)} %div.14, f32[]{:T(128)S(6)} %div.12, f32[]{:T(128)S(6)} %div.13, f32[1,512,4096]{1,2,0:T(8,128)} %get-tuple-element.46), kind=kLoop, calls=%fused_computation.12 | loop fusion | flops 16777216 | bytes 20971532 | tf_op jit(solution)/shard_map/add | solution.py:90
  527.6 8.9 %copy.45 = f32[1,512,4096]{2,1,0:T(8,128)} copy(f32[1,512,4096]{1,2,0:T(8,128)} %fusion.4) | data formatting | bytes 16777216
  (16 shorter events, 0.3 us)
Async XLA Ops:
  7.2 1.1 copy-start
  7.2 107.4 %reduce-scatter.5.cloned.1.call-start = ((), (), s32[]{:S(2)}) async-start(), calls=%async_computation.6 | async-start | bytes 13369344 | tf_op jit(solution)/shard_map/reduce_scatter | solution.py:72
  16.9 104.4 %copy-start.1 = (s32[16,2]{0,1:T(2,128)S(1)}, s32[16,2]{0,1:T(2,128)}, u32[]{:S(2)}) copy-start(s32[16,2]{0,1:T(2,128)} %param.8) | copy-start | bytes 388
  16.9 105.0 %copy-start.3 = (f32[16,2]{0,1:T(2,128)S(1)}, f32[16,2]{0,1:T(2,128)}, u32[]{:S(2)}) copy-start(f32[16,2]{0,1:T(2,128)} %param.9) | copy-start | bytes 388
  16.9 120.4 %copy-start.2 = (f32[16]{0:T(128)S(1)}, f32[16]{0:T(128)}, u32[]{:S(2)}) copy-start(f32[16]{0:T(128)} %param.10) | copy-start | bytes 196
  116.7 20.4 %all-to-all-start = ((f32[8,6,4096]{2,1,0:T(8,128)}), f32[8,6,4096]{2,1,0:T(8,128)S(1)}, u32[]{:S(2)}, u32[]{:S(2)}) async-start(f32[8,6,4096]{2,1,0:T(8,128)} %all_to_all.32), calls=%async_computation.1 | async-start | bytes 2097152 | tf_op jit(solution)/shard_map/all_to_all | solution.py:78
  121.2 89.5 %all-gather.3.cloned.1.call-start = ((), (), s32[]{:S(2)}) async-start(), calls=%async_computation.7 | async-start | bytes 6684672 | tf_op jit(solution)/shard_map/all_gather | solution.py:83
  152.4 225.0 %reduce-scatter.7.cloned.1.call-start = ((), (), s32[]{:S(2)}) async-start(), calls=%async_computation.9 | async-start | bytes 13369344 | tf_op jit(solution)/shard_map/reduce_scatter | solution.py:72
  287.5 184.9 %all-gather.5.cloned.1.call-start = ((), (), s32[]{:S(2)}) async-start(), calls=%async_computation.8 | async-start | bytes 6684672 | tf_op jit(solution)/shard_map/all_gather | solution.py:83
Sparse Core Ops, SparseCore 0:
  17.0 97.4 reduce-scatter.4
  152.5 58.1 all-gather.2
  287.6 89.6 reduce-scatter.6
  414.2 58.1 all-gather.4
where the time goes:
time: 545 us; the launch traced here: 544 us
  waiting for transfers between devices  297 us (54%)
  blocking collectives  116 us (21%)
  matrix products  46.6 us (9%)
  local copies, waits for them, and re-layouts  41.8 us (8%)
  between operations  22 us (4%)
  other arithmetic  16.5 us (3%)
    reduce_scatter x2, waiting for transfers between devices, local(): lax.psum_scatter(jnp.dot(local_hidden, rounded, preferred_element_type=jn...  187 us
    all_gather x2, waiting for transfers between devices, local(): lax.all_gather(returned, FSDP, axis=0, tiled=True)  94.5 us
    psum x8, blocking collectives, by_axis(): array = lax.psum(array, axis)  69.9 us
    unnamed x13, local copies, waits for them, and re-layouts  35.8 us
    all_to_all x2, blocking collectives, local(): lax.all_to_all(leaving, EXPERT, split_axis=0, concat_axis=0, tiled=True)  25.5 us
    dot_general x2, matrix products, local(): lax.dot_general(local_hidden, lax.all_gather(returned, FSDP, axis=0, tile...  22.3 us
    dot_general x2, matrix products, local(): jnp.dot(local_hidden, rounded, preferred_element_type=jnp.float32)  21.6 us
    all_to_all x1, blocking collectives, local(): lax.all_to_all(summed, EXPERT, split_axis=0, concat_axis=0, tiled=True)  20.2 us
  transfers between devices with their start and end apart: 5, of which 5 were waited for; matrix products, arithmetic and copies ran while one was open for 4% of the time, Pallas kernels for 0%

commit v1 on v0

--- a/solution.py
+++ b/solution.py
@@ -14,7 +14,7 @@
 
 def by_axis(array, axes):
     for axis in axes:
-        array = lax.psum(array, axis)
+        array = jnp.sum(lax.all_gather(array, axis), axis=0)
     return array
 
 

time: 545 us -> 595 us (1.092)
  local copies, waits for them, and re-layouts: 41.8 us -> 83.5 us
  other arithmetic: 16.5 us -> 33.9 us
  blocking collectives: 116 us -> 110 us
    psum x8 -> x0, blocking collectives: 69.9 us -> none  [by_axis(): array = lax.psum(array, axis)]
    unnamed x0 -> x8, blocking collectives: none -> 64.3 us
    unnamed x13 -> x81, local copies, waits for them, and re-layouts: 35.8 us -> 77.5 us
    reduce_sum x0 -> x28, other arithmetic: none -> 17.4 us  [by_axis(): array = jnp.sum(lax.all_gather(array, axis), axis=0)]
  transfers between devices with their start and end apart: 5 -> 5, of which waited for: 5 -> 5; matrix products, arithmetic and copies ran while one was open for 4% -> 5% of each run, Pallas kernels for 0% -> 0%
where the time goes in v1:
time: 595 us; the launch traced here: 593 us
  waiting for transfers between devices  292 us (49%)
  blocking collectives  110 us (18%)
  local copies, waits for them, and re-layouts  83.5 us (14%)
  matrix products  46.6 us (8%)
  other arithmetic  33.9 us (6%)
  between operations  22.2 us (4%)
    reduce_scatter x2, waiting for transfers between devices, local(): lax.psum_scatter(jnp.dot(local_hidden, rounded, preferred_element_type=jn...  188 us
    all_gather x2, waiting for transfers between devices, local(): lax.all_gather(returned, FSDP, axis=0, tiled=True)  89.5 us
    unnamed x81, local copies, waits for them, and re-layouts  77.5 us
    unnamed x8, blocking collectives  64.3 us
    all_to_all x2, blocking collectives, local(): lax.all_to_all(leaving, EXPERT, split_axis=0, concat_axis=0, tiled=True)  25.5 us
    dot_general x2, matrix products, local(): lax.dot_general(local_hidden, lax.all_gather(returned, FSDP, axis=0, tile...  22.4 us
    dot_general x2, matrix products, local(): jnp.dot(local_hidden, rounded, preferred_element_type=jnp.float32)  21.6 us
    all_to_all x1, blocking collectives, local(): lax.all_to_all(summed, EXPERT, split_axis=0, concat_axis=0, tiled=True)  20.2 us
  transfers between devices with their start and end apart: 5, of which 5 were waited for; matrix products, arithmetic and copies ran while one was open for 5% of the time, Pallas kernels for 0%

profile of v1, /device:TPU:0, one launch (start us, length us, event | category | flops | bytes accessed | tf_op | source)
XLA Modules:
  0.0 593.4 jit_solution(5223426219740897996)
XLA Ops:
  8.3 8.6 %fusion.10 = f32[768,4096]{1,0:T(8,128)} fusion(bf16[1,512,4096]{2,1,0:T(8,128)(2,1)} %param.12, bf16[1,768,512]{2,1,0:T(8,128)(2,1)S(1)} %copy-done), kind=kOutput, calls=%fused_computation.26 | convolution fusion | flops 3221225472 | bytes 17563648 | tf_op jit(solution)/shard_map/dot_general | solution.py:73
  16.9 97.7 %reduce-scatter.5.cloned.1.call-done = f32[48,4096]{1,0:T(8,128)} async-done(((f32[768,4096]{1,0:T(8,128)}), f32[48,4096]{1,0:T(8,128)}) %reduce-scatter.5.cloned.1.call-update) | async-done | bytes 786448 | tf_op jit(solution)/shard_map/reduce_scatter | solution.py:72
  114.5 2.2 all_to_all.32
  116.7 4.6 all-to-all-start
  122.1 15.1 %all-to-all-done = f32[8,6,4096]{2,1,0:T(8,128)S(1)} async-done(((f32[8,6,4096]{2,1,0:T(8,128)}), f32[8,6,4096]{2,1,0:T(8,128)S(1)}, u32[]{:S(2)}, u32[]{:S(2)}) %all-to-all-start) | async-done | bytes 786464 | tf_op jit(solution)/shard_map/all_to_all | solution.py:78
  138.8 12.8 %all_to_all.48 = bf16[8,6,4096]{2,1,0:T(8,128)(2,1)S(1)} all-to-all(bf16[8,6,4096]{2,1,0:T(8,128)(2,1)S(1)} %all_to_all.35), channel_id=1, replica_groups=mesh['expert_0'=4,'expert_1'=2,'fsdp_0'=4,'fsdp_1'=4] {'expert_0','exper..., dimensions={0} | all-to-all | bytes 786432 | tf_op jit(solution)/shard_map/all_to_all | solution.py:80
  152.6 6.5 %copy.40 = bf16[1,512,4096]{1,2,0:T(8,128)(2,1)} copy(bf16[1,512,4096]{2,1,0:T(8,128)(2,1)} %param.12) | data formatting | bytes 8388608 | tf_op args[5]
  160.4 50.5 %all-gather.3.cloned.1.call-done = bf16[768,4096]{1,0:T(8,128)(2,1)} async-done(((bf16[48,4096]{1,0:T(8,128)(2,1)}), bf16[768,4096]{1,0:T(8,128)(2,1)}) %all-gather.3.cloned.1.call-update) | async-done | bytes 6291472 | tf_op jit(solution)/shard_map/all_gather | solution.py:83
  210.8 12.3 %multiply_reduce_fusion = (f32[]{:T(128)}, f32[]{:T(128)}, f32[]{:T(128)}, f32[1,512,4096]{1,2,0:T(8,128)}) fusion(bf16[1,512,4096]{1,2,0:T(8,128)(2,1)} %copy.40, f32[]{:T(128)} %bitcast.76, bf16[768,4096]{1,0:T(8,128)(2,1)} %all-gather.3.cloned.1.call-done, bf16[1,768,512]{2,1,0:T(8,128)(2,1)S(1)} %copy-done), kind=kOutput, calls=%fused_computation.18 | convolution fusion | flops 3240099840 | bytes 19660816 | tf_op jit(solution)/shard_map/dot_general | solution.py:81
  223.1 1.4 dynamic-update-slice
  225.9 1.4 dynamic-update-slice.4
  227.9 10.7 %all-reduce.33 = (f32[4]{0:T(128)S(1)}, f32[4]{0:T(128)S(1)}, f32[4]{0:T(128)S(1)}) all-reduce(f32[4]{0:T(128)S(1)} %dynamic-update-slice, f32[4]{0:T(128)S(1)} %dynamic-update-slice.4, f32[4]{0:T(128)S(1)} %dynamic-update-slice.12), channel_id=1, replica_groups=mesh['expert_0'=4,'expert_1'=2,'fsdp_0'=4,'fsdp_1'=4] {'expert_0'}, use_global_device_ids=true, to_apply=%add | all-reduce | flops 12 | bytes 96
  241.1 1.4 dynamic-update-slice.5
  243.2 1.4 dynamic-update-slice.1
  245.3 2.4 all-reduce.35
  250.3 1.5 dynamic-update-slice.6
  252.5 1.5 dynamic-update-slice.2
  254.7 10.4 %all-reduce.31 = (f32[4]{0:T(128)S(1)}, f32[4]{0:T(128)S(1)}, f32[4]{0:T(128)S(1)}) all-reduce(f32[4]{0:T(128)S(1)} %dynamic-update-slice.2, f32[4]{0:T(128)S(1)} %dynamic-update-slice.6, f32[4]{0:T(128)S(1)} %dynamic-update-slice.14), channel_id=1, replica_groups=mesh['expert_0'=4,'expert_1'=2,'fsdp_0'=4,'fsdp_1'=4] {'fsdp_0'}, use_global_device_ids=true, to_apply=%add.2 | all-reduce | flops 12 | bytes 96
  267.6 1.4 dynamic-update-slice.7
  269.7 1.4 dynamic-update-slice.3
  271.1 8.7 %all-reduce.29 = (f32[4]{0:T(128)S(1)}, f32[4]{0:T(128)S(1)}, f32[4]{0:T(128)S(1)}) all-reduce(f32[4]{0:T(128)S(1)} %dynamic-update-slice.3, f32[4]{0:T(128)S(1)} %dynamic-update-slice.7, f32[4]{0:T(128)S(1)} %dynamic-update-slice.15), channel_id=1, replica_groups=mesh['expert_0'=4,'expert_1'=2,'fsdp_0'=4,'fsdp_1'=4] {'fsdp_1'}, use_global_device_ids=true, to_apply=%add.3 | all-reduce | flops 12 | bytes 96
  285.6 13.1 %convolution_bitcast_fusion = f32[768,4096]{0,1:T(8,128)} fusion(bf16[1,768,512]{2,1,0:T(8,128)(2,1)S(1)} %copy-done, bf16[1,512,4096]{1,2,0:T(8,128)(2,1)} %copy.40, f32[1,512,4096]{1,2,0:T(8,128)} %get-tuple-element.46, f32[]{:T(128)S(6)} %div.13, f32[]{:T(128)S(6)} %div.12), kind=kOutput, calls=%fused_computation.20 | convolution fusion | flops 3233808384 | bytes 25952264 | tf_op jit(solution)/shard_map/dot_general | solution.py:73
  298.6 12.6 %copy.46 = f32[768,4096]{1,0:T(8,128)} copy(f32[768,4096]{0,1:T(8,128)} %convolution_bitcast_fusion) | data formatting | bytes 25165824
  311.3 90.0 %reduce-scatter.7.cloned.1.call-done = f32[48,4096]{1,0:T(8,128)} async-done(((f32[768,4096]{1,0:T(8,128)}), f32[48,4096]{1,0:T(8,128)}) %reduce-scatter.7.cloned.1.call-update) | async-done | bytes 786448 | tf_op jit(solution)/shard_map/reduce_scatter | solution.py:72
  402.6 20.2 %all_to_all.49 = f32[8,6,4096]{2,1,0:T(8,128)S(1)} all-to-all(f32[8,6,4096]{2,1,0:T(8,128)S(1)} %all_to_all.38), channel_id=1, replica_groups=mesh['expert_0'=4,'expert_1'=2,'fsdp_0'=4,'fsdp_1'=4] {'expert_0','exper..., dimensions={0} | all-to-all | bytes 1572864 | tf_op jit(solution)/shard_map/all_to_all | solution.py:78
  424.4 12.8 %all_to_all.50 = bf16[8,6,4096]{2,1,0:T(8,128)(2,1)S(1)} all-to-all(bf16[8,6,4096]{2,1,0:T(8,128)(2,1)S(1)} %all_to_all.41), channel_id=1, replica_groups=mesh['expert_0'=4,'expert_1'=2,'fsdp_0'=4,'fsdp_1'=4] {'expert_0','exper..., dimensions={0} | all-to-all | bytes 786432 | tf_op jit(solution)/shard_map/all_to_all | solution.py:80
  438.1 6.6 %copy.44 = bf16[1,512,4096]{1,2,0:T(8,128)(2,1)} copy(bf16[1,512,4096]{2,1,0:T(8,128)(2,1)} %param.13) | data formatting | bytes 8388608 | tf_op args[6]
  444.6 8.4 %fusion = (f32[]{:T(128)}, f32[]{:T(128)}, f32[]{:T(128)}) fusion(bf16[1,512,4096]{1,2,0:T(8,128)(2,1)} %copy.44, f32[]{:T(128)S(6)} %div.13, f32[1,512,4096]{1,2,0:T(8,128)} %get-tuple-element.46, f32[]{:T(128)S(6)} %div.12, bf16[1,512,4096]{1,2,0:T(8,128)(2,1)} %copy.40), kind=kLoop, calls=%fused_computation.8 | loop fusion | flops 25165824 | bytes 16777236 | tf_op jit(solution)/shard_map/reduce_sum | solution.py:51
  453.0 1.5 dynamic-update-slice.20
  455.8 1.4 dynamic-update-slice.8
  457.3 39.1 %all-gather.5.cloned.1.call-done = bf16[768,4096]{1,0:T(8,128)(2,1)} async-done(((bf16[48,4096]{1,0:T(8,128)(2,1)}), bf16[768,4096]{1,0:T(8,128)(2,1)}) %all-gather.5.cloned.1.call-update) | async-done | bytes 6291472 | tf_op jit(solution)/shard_map/all_gather | solution.py:83
  496.3 10.1 %fusion.8 = f32[]{:T(128)} fusion(bf16[768,4096]{1,0:T(8,128)(2,1)} %all-gather.5.cloned.1.call-done, f32[]{:T(128)} %bitcast.77, bf16[1,768,512]{2,1,0:T(8,128)(2,1)S(1)} %copy-done, f32[]{:T(128)S(6)} %div.13, f32[1,512,4096]{1,2,0:T(8,128)} %get-tuple-element.46, f32[]{:T(128)S(6)} %div.12, bf16[1,512,4096]{1,2,0:T(8,128)(2,1)} %copy.40), kind=kOutput, calls=%fused_computation.17 | convolution fusion | flops 3240099840 | bytes 19660816 | tf_op jit(solution)/shard_map/dot_general | solution.py:81
  507.8 10.7 %all-reduce.32 = (f32[4]{0:T(128)S(1)}, f32[4]{0:T(128)S(1)}, f32[4]{0:T(128)S(1)}, f32[4]{0:T(128)S(1)}) all-reduce(f32[4]{0:T(128)S(1)} %dynamic-update-slice.8, f32[4]{0:T(128)S(1)} %dynamic-update-slice.16, f32[4]{0:T(128)S(1)} %dynamic-update-slice.20, ...), channel_id=1, replica_groups=mesh['expert_0'=4,'expert_1'=2,'fsdp_0'=4,'fsdp_1'=4] {'expert_0'}, use_global_device_ids=true, to_apply=%add.8 | all-reduce | flops 16 | bytes 128
  519.0 1.5 dynamic-update-slice.21
  521.1 1.4 dynamic-update-slice.25
  526.4 2.4 all-reduce.34
  529.5 1.4 dynamic-update-slice.22
  531.5 1.4 dynamic-update-slice.26
  533.6 1.4 dynamic-update-slice.18
  535.6 1.4 dynamic-update-slice.10
  537.1 10.4 %all-reduce.30 = (f32[4]{0:T(128)S(1)}, f32[4]{0:T(128)S(1)}, f32[4]{0:T(128)S(1)}, f32[4]{0:T(128)S(1)}) all-reduce(f32[4]{0:T(128)S(1)} %dynamic-update-slice.10, f32[4]{0:T(128)S(1)} %dynamic-update-slice.18, f32[4]{0:T(128)S(1)} %dynamic-update-slice.22, ...), channel_id=1, replica_groups=mesh['expert_0'=4,'expert_1'=2,'fsdp_0'=4,'fsdp_1'=4] {'fsdp_0'}, use_global_device_ids=true, to_apply=%add.10 | all-reduce | flops 16 | bytes 128
  548.1 1.4 dynamic-update-slice.23
  550.0 1.4 dynamic-update-slice.27
  552.0 1.4 dynamic-update-slice.19
  554.0 1.4 dynamic-update-slice.11
  555.4 8.6 %all-reduce.28 = (f32[4]{0:T(128)S(1)}, f32[4]{0:T(128)S(1)}, f32[4]{0:T(128)S(1)}, f32[4]{0:T(128)S(1)}) all-reduce(f32[4]{0:T(128)S(1)} %dynamic-update-slice.11, f32[4]{0:T(128)S(1)} %dynamic-update-slice.19, f32[4]{0:T(128)S(1)} %dynamic-update-slice.23, ...), channel_id=1, replica_groups=mesh['expert_0'=4,'expert_1'=2,'fsdp_0'=4,'fsdp_1'=4] {'fsdp_1'}, use_global_device_ids=true, to_apply=%add.11 | all-reduce | flops 16 | bytes 128
  566.6 7.7 %fusion.4 = f32[1,512,4096]{1,2,0:T(8,128)} fusion(bf16[1,512,4096]{1,2,0:T(8,128)(2,1)} %copy.40, f32[]{:T(128)S(6)} %div.14, f32[]{:T(128)S(6)} %div.12, f32[]{:T(128)S(6)} %div.13, f32[1,512,4096]{1,2,0:T(8,128)} %get-tuple-element.46), kind=kLoop, calls=%fused_computation.12 | loop fusion | flops 16777216 | bytes 20971532 | tf_op jit(solution)/shard_map/add | solution.py:90
  576.8 8.9 %copy.45 = f32[1,512,4096]{2,1,0:T(8,128)} copy(f32[1,512,4096]{1,2,0:T(8,128)} %fusion.4) | data formatting | bytes 16777216
  (112 shorter events, 38.9 us)
Async XLA Ops:
  7.2 1.1 copy-start
  7.2 107.4 %reduce-scatter.5.cloned.1.call-start = ((), (), s32[]{:S(2)}) async-start(), calls=%async_computation.6 | async-start | bytes 13369344 | tf_op jit(solution)/shard_map/reduce_scatter | solution.py:72
  16.9 104.5 %copy-start.1 = (s32[16,2]{0,1:T(2,128)S(1)}, s32[16,2]{0,1:T(2,128)}, u32[]{:S(2)}) copy-start(s32[16,2]{0,1:T(2,128)} %param.8) | copy-start | bytes 388
  16.9 105.2 %copy-start.3 = (f32[16,2]{0,1:T(2,128)S(1)}, f32[16,2]{0,1:T(2,128)}, u32[]{:S(2)}) copy-start(f32[16,2]{0,1:T(2,128)} %param.9) | copy-start | bytes 388
  16.9 120.5 %copy-start.2 = (f32[16]{0:T(128)S(1)}, f32[16]{0:T(128)}, u32[]{:S(2)}) copy-start(f32[16]{0:T(128)} %param.10) | copy-start | bytes 196
  116.7 43.0 %copy-start.7 = (u32[128]{0:T(128)S(1)}, u32[128]{0:T(128)}, u32[]{:S(2)}) copy-start(u32[128]{0:T(128)} %constant.24) | copy-start | bytes 1540
  116.7 20.5 %all-to-all-start = ((f32[8,6,4096]{2,1,0:T(8,128)}), f32[8,6,4096]{2,1,0:T(8,128)S(1)}, u32[]{:S(2)}, u32[]{:S(2)}) async-start(f32[8,6,4096]{2,1,0:T(8,128)} %all_to_all.32), calls=%async_computation.1 | async-start | bytes 2097152 | tf_op jit(solution)/shard_map/all_to_all | solution.py:78
  121.3 89.5 %all-gather.3.cloned.1.call-start = ((), (), s32[]{:S(2)}) async-start(), calls=%async_computation.7 | async-start | bytes 6684672 | tf_op jit(solution)/shard_map/all_gather | solution.py:83
  152.5 248.9 %reduce-scatter.7.cloned.1.call-start = ((), (), s32[]{:S(2)}) async-start(), calls=%async_computation.9 | async-start | bytes 13369344 | tf_op jit(solution)/shard_map/reduce_scatter | solution.py:72
  210.8 16.5 %copy-start.6 = (u32[128]{0:T(128)S(1)}, u32[128]{0:T(128)}, u32[]{:S(2)}) copy-start(u32[128]{0:T(128)} %constant.29) | copy-start | bytes 1540
  210.8 33.8 %copy-start.5 = (u32[128]{0:T(128)S(1)}, u32[128]{0:T(128)}, u32[]{:S(2)}) copy-start(u32[128]{0:T(128)} %constant.34) | copy-start | bytes 1540
  210.8 43.2 %copy-start.4 = (u32[128]{0:T(128)S(1)}, u32[128]{0:T(128)}, u32[]{:S(2)}) copy-start(u32[128]{0:T(128)} %constant.39) | copy-start | bytes 1540
  311.3 185.0 %all-gather.5.cloned.1.call-start = ((), (), s32[]{:S(2)}) async-start(), calls=%async_computation.8 | async-start | bytes 6684672 | tf_op jit(solution)/shard_map/all_gather | solution.py:83
Sparse Core Ops, SparseCore 0:
  17.0 97.4 reduce-scatter.4
  152.6 58.1 all-gather.2
  311.4 89.9 reduce-scatter.6
  438.2 58.0 all-gather.4
